TPU v7x, 32 devices: a whole 2x2x4 slice. The times are simulated.
32 devices in a mesh: row: 4 (over y, core), col: 8 (over z, x).
Axes of the slice: x: 2, y: 2, z: 4, core: 2. Of those that a mesh axis runs over, the one named last changes fastest.
Arguments:
- fock: float32 [2, 8192, 8192], P(None, 'row', 'col'), may hold values from -1.1875 to 1.1875, as said below
- density: float32 [2, 8192, 8192], P(None, 'row', 'col'), may hold values from -1.09375 to 1.09375, as said below
- probe: float32 [2, 8192, 128], P(None, 'col'), may hold values from -6 to 6
Outputs:
- propagated: float32 [2, 8192, 128], P(None, 'col')
Inputs may be any that keep to these rules, and one draw needn't show every extreme that they name: Hermitian: fock[0] is symmetric and fock[1] antisymmetric, exactly. Hermitian: density[0] is symmetric and density[1] antisymmetric, exactly.
All inputs are finite; a program needn't handle non-finite values.
Results may differ from a plain program's by a relative error of at most 0.00011.
Values sent between devices are 32-bit elements; how exact they have to be, the bound alone decides.
A program may use at most 128 MiB of HBM per device.

v0:
```python
import functools

import jax
import jax.numpy as jnp
from jax import lax
from jax.experimental import pallas as pl
from jax.experimental.pallas import tpu as pltpu
from jax.sharding import PartitionSpec as P

time_step = 0.5
MESH = pl.DeviceIdType.MESH


def split(value):
    high = value.astype(jnp.bfloat16)
    return high, (value - high.astype(jnp.float32)).astype(jnp.bfloat16)


def dot3(left, right):
    dot = functools.partial(jnp.dot, preferred_element_type=jnp.float32)
    return dot(left[0], right[0]) + (dot(left[0], right[1]) + dot(left[1], right[0]))


def kernel(
    nr, nc, fock_hbm, density_hbm, probe_ref, out_ref,
    fock, density, high, low, base,
    send1, recv1, gather1, turned, flat, recv2, gather2, send3, recv3, moved, gather4,
    fock_sem, density_sem, own_sem,
    s1, r1, s2, r2, s3, r3, s4, r4, s5, r5, s6, r6, s7, r7,
):
    r = lax.axis_index("row")
    c = lax.axis_index("col")
    rows = fock.shape[1]
    cols = fock.shape[2]
    m = probe_ref.shape[2]
    s = rows // nc
    half = nc // 2
    side = lax.div(c, half)
    spot = lax.rem(c, half)

    def block_to(e):
        return lax.rem(side + 1 + e // half, 2) * half + lax.rem(spot + 1 + e % half, half)

    def block_from(e):
        return lax.rem(side + 1 + e // half, 2) * half + lax.rem(spot + half - 1 - e % half, half)

    def near(e):
        return side * half + lax.rem(spot + 1 + e % half, half)

    across = lax.rem(side + 1, 2) * half + spot

    def at(block):
        return pl.ds(pl.multiple_of(block * s, s), s)

    def peer_to(me, d, n):
        return lax.rem(me + 1 + d, n)

    def peer_from(me, d, n):
        return lax.rem(me + 2 * n - 1 - d, n)

    def fock_load(d):
        block = block_to(d)
        return pltpu.make_async_copy(
            fock_hbm.at[:, at(block), :], fock.at[:, at(block), :], fock_sem.at[d]
        )

    def density_load(d):
        block = block_from(d)
        return pltpu.make_async_copy(
            density_hbm.at[:, at(block), :], density.at[:, at(block), :], density_sem.at[d]
        )

    def each(n, body):
        def step(d, carry):
            body(d)
            return carry

        lax.fori_loop(0, n, step, 0)

    each(nc, lambda d: fock_load(d).start())
    density_load(nc - 1).start()
    density_load(half - 1).start()
    each(half - 1, lambda d: density_load(half + d).start())
    each(half - 1, lambda d: density_load(d).start())

    mine = nc * r + c
    wanted = nr * c + r
    goal = (lax.rem(mine, nr), lax.div(mine, nr))
    stays = mine == wanted

    barrier = pltpu.get_barrier_semaphore()

    def greet(where):
        pl.semaphore_signal(barrier, inc=1, device_id=where, device_id_type=MESH)

    def greet_next(d):
        other = lax.rem(mine + 1 + d, nr * nc)
        greet((lax.div(other, nc), lax.rem(other, nc)))

    each(nr * nc - 1, greet_next)

    base[:, :m] = probe_ref[0]
    base[:, m:] = probe_ref[1]
    top, rest = split(base[...])
    high[...] = top
    low[...] = rest

    pl.semaphore_wait(barrier, nr * nc - 1)

    def col_copy(e, where, source, target, ssem, rsem):
        return pltpu.make_async_remote_copy(
            src_ref=source, dst_ref=target.at[e], send_sem=ssem.at[e], recv_sem=rsem.at[e],
            device_id=(r, where), device_id_type=MESH,
        )

    def row_copy(d, source, target, ssem, rsem):
        return pltpu.make_async_remote_copy(
            src_ref=source, dst_ref=target.at[d], send_sem=ssem.at[d], recv_sem=rsem.at[d],
            device_id=(peer_to(r, d, nr), c), device_id_type=MESH,
        )

    def forward(block, factor):
        right = (high[...], low[...])
        one = dot3(split(fock[0, at(block), :]), right)
        two = dot3(split(fock[1, at(block), :]), right)
        real = one[:, :m] - two[:, m:]
        imag = one[:, m:] + two[:, :m]
        piece = nc * r + block
        weight = jnp.where(lax.div(piece, nr) == c, 1.0, 0.0).astype(jnp.float32)
        own = base[at(lax.rem(piece, nr)), :] * weight
        return own[:, :m] - factor * imag, own[:, m:] + factor * real

    def forward_reduce(factor, load, send, recv, ssem, rsem):
        def product(e, target):
            if load:
                fock_load(e).wait()
            real, imag = forward(block_to(e), factor)
            target[e, :, :m] = real
            target[e, :, m:] = imag

        def partial_copy(e):
            return col_copy(e, near(e), send.at[e], recv, ssem, rsem)

        def sum_copy():
            return col_copy(half - 1, across, recv.at[half - 1], send, ssem, rsem)

        def step(e):
            product(e, send)
            partial_copy(e).start()

        def take(e, total):
            partial_copy(e).wait_recv()
            recv[total] += recv[e]

        each(half - 1, step)
        product(half - 1, recv)
        each(half - 1, lambda d: step(half + d))
        product(nc - 1, recv)
        each(half - 1, lambda d: take(d, half - 1))
        sum_copy().start()
        each(half - 1, lambda d: take(half + d, nc - 1))
        sum_copy().wait_recv()
        recv[nc - 1] += send[half - 1]

        def drain():
            each(half - 1, lambda d: partial_copy(d).wait_send())
            each(half - 1, lambda d: partial_copy(half + d).wait_send())
            sum_copy().wait_send()

        return drain

    drain1 = forward_reduce(time_step, True, send1, recv1, s1, r1)

    gather1[nc - 1] = recv1[nc - 1]
    def across_copy():
        return col_copy(half - 1, across, gather1.at[nc - 1], gather1, s2, r2)

    def near_copy(d):
        return col_copy(half + d, near(d), gather1.at[nc - 1], gather1, s2, r2)

    def forward_copy(d):
        return col_copy(d, near(d), gather1.at[half - 1], gather1, s2, r2)

    across_copy().start()
    each(half - 1, lambda d: near_copy(d).start())

    def backward(e):
        density_load(e).wait()
        block = block_from(e)
        left = split(gather1[e].T)
        one = dot3(left, split(density[0, at(block), :]))
        two = dot3(left, split(density[1, at(block), :]))
        return one[:m] + two[m:], one[m:] - two[:m]

    real, imag = backward(nc - 1)
    turned[:m] = real
    turned[m:] = imag

    across_copy().wait_recv()
    each(half - 1, lambda d: forward_copy(d).start())

    def add_backward(e):
        real, imag = backward(e)
        turned[:m] += real
        turned[m:] += imag

    def gathered_near(d):
        near_copy(d).wait_recv()
        add_backward(half + d)

    def gathered_far(d):
        forward_copy(d).wait_recv()
        add_backward(d)

    add_backward(half - 1)
    each(half - 1, gathered_near)
    each(half - 1, gathered_far)
    flat[...] = turned[...].T

    each(nr - 1, lambda d: row_copy(d, flat.at[at(peer_to(r, d, nr)), :], recv2, s3, r3).start())
    recv2[nr - 1] = flat[at(r), :]

    def take_row(d):
        row_copy(d, flat.at[at(peer_to(r, d, nr)), :], recv2, s3, r3).wait_recv()
        recv2[nr - 1] += recv2[d]

    each(nr - 1, take_row)

    gather2[nr - 1] = recv2[nr - 1]
    each(nr - 1, lambda d: row_copy(d, gather2.at[nr - 1], gather2, s4, r4).start())

    def place(slot):
        value = gather2[slot]
        where = at(peer_from(r, slot, nr))
        top, rest = split(value)
        base[where, :] = value
        high[where, :] = top
        low[where, :] = rest

    place(nr - 1)

    def take_vector(d):
        row_copy(d, gather2.at[nr - 1], gather2, s4, r4).wait_recv()
        place(d)

    each(nr - 1, take_vector)

    drain3 = forward_reduce(-time_step, False, send3, recv3, s5, r5)

    moved[...] = recv3[nc - 1]

    def move():
        return pltpu.make_async_remote_copy(
            src_ref=moved, dst_ref=gather4.at[nr - 1], send_sem=s6.at[0], recv_sem=r6.at[0],
            device_id=goal, device_id_type=MESH,
        )

    def stay():
        return pltpu.make_async_copy(moved, gather4.at[nr - 1], own_sem.at[0])

    @pl.when(stays)
    def _():
        stay().start()
        stay().wait()

    @pl.when(jnp.logical_not(stays))
    def _():
        move().start()
        move().wait()

    each(nr - 1, lambda d: row_copy(d, gather4.at[nr - 1], gather4, s7, r7).start())

    def emit(slot):
        where = at(peer_from(r, slot, nr))
        out_ref[0, where, :] = gather4[slot, :, :m]
        out_ref[1, where, :] = gather4[slot, :, m:]

    emit(nr - 1)

    def take_out(d):
        row_copy(d, gather4.at[nr - 1], gather4, s7, r7).wait_recv()
        emit(d)

    each(nr - 1, take_out)

    drain1()
    drain3()
    across_copy().wait_send()
    each(half - 1, lambda d: near_copy(d).wait_send())
    each(half - 1, lambda d: forward_copy(d).wait_send())

    def drain_row(d):
        row_copy(d, flat.at[at(peer_to(r, d, nr)), :], recv2, s3, r3).wait_send()
        row_copy(d, gather2.at[nr - 1], gather2, s4, r4).wait_send()
        row_copy(d, gather4.at[nr - 1], gather4, s7, r7).wait_send()

    each(nr - 1, drain_row)


def solution(mesh):
    nr = mesh.shape["row"]
    nc = mesh.shape["col"]

    def shards(fock, density, probe):
        _, rows, cols = fock.shape
        m = probe.shape[2]
        s = rows // nc
        f32 = jnp.float32
        vmem = pltpu.VMEM
        sem = pltpu.SemaphoreType.DMA
        many, few = (nc, s, 2 * m), (nr, s, 2 * m)
        return pl.pallas_call(
            functools.partial(kernel, nr, nc),
            out_shape=jax.ShapeDtypeStruct(probe.shape, f32),
            in_specs=[
                pl.BlockSpec(memory_space=pl.ANY),
                pl.BlockSpec(memory_space=pl.ANY),
                pl.BlockSpec(memory_space=pltpu.VMEM),
            ],
            out_specs=pl.BlockSpec(memory_space=pltpu.VMEM),
            scratch_shapes=[
                vmem(fock.shape, f32),
                vmem(density.shape, f32),
                vmem((cols, 2 * m), jnp.bfloat16),
                vmem((cols, 2 * m), jnp.bfloat16),
                vmem((cols, 2 * m), f32),
                vmem(many, f32),
                vmem(many, f32),
                vmem(many, f32),
                vmem((2 * m, cols), f32),
                vmem((cols, 2 * m), f32),
                vmem(few, f32),
                vmem(few, f32),
                vmem(many, f32),
                vmem(many, f32),
                vmem((s, 2 * m), f32),
                vmem(few, f32),
                sem((nc,)),
                sem((nc,)),
                sem((1,)),
                *[sem((nc,))] * 14,
            ],
            compiler_params=pltpu.CompilerParams(
                collective_id=0, has_side_effects=True, vmem_limit_bytes=62 * 1024 * 1024
            ),
            name="propagate",
        )(fock, density, probe)

    return jax.shard_map(
        shards,
        mesh=mesh,
        in_specs=(P(None, "row", "col"), P(None, "row", "col"), P(None, "col", None)),
        out_specs=P(None, "col", None),
        check_vma=False,
    )
```

profile of v0, /device:TPU:15, one launch (start us, length us, event | category | flops | bytes accessed | tf_op | source)
XLA Modules:
  0.0 149.7 jit_solution(16175481446192699773)
XLA Ops:
  0.0 147.4 %propagate.1 = f32[2,1024,128]{2,1,0:T(8,128)} custom-call(f32[2,2048,1024]{2,1,0:T(8,128)} %fock_hbm.1, f32[2,2048,1024]{2,1,0:T(8,128)} %density_hbm.1, f32[2,1024,128]{2,1,0:T(8,128)} %probe_ref.1), custom_call_target="tpu_custom_call" | custom-call | tf_op jit(solution)/shard_map/propagate/pallas_call | solution.py:312
  147.4 2.3 %copy.5 = f32[2,1024,128]{2,1,0:T(8,128)} copy(f32[2,1024,128]{2,1,0:T(8,128)} %propagate.1) | data formatting | bytes 2097152
where the time goes:
time: 150 us
  Pallas kernels  147 us (98%)
  local copies, waits for them, and re-layouts  2.26 us (2%)
    pallas_call x1, Pallas kernels, shards(): pl.pallas_call(functools.partial(kernel, nr, nc), out_shape=jax.ShapeDtyp...  147 us

commit v1 on v0

v1 whole, which is shorter than its diff:
```python
import functools

import jax
import jax.numpy as jnp
from jax import lax
from jax.experimental import pallas as pl
from jax.experimental.pallas import tpu as pltpu
from jax.sharding import PartitionSpec as P

time_step = 0.5
MESH = pl.DeviceIdType.MESH
GROUPS = 4
STAGES = 3
CORES = 2
SLOTS = 4


def split(value):
    high = value.astype(jnp.bfloat16)
    return high, (value - high.astype(jnp.float32)).astype(jnp.bfloat16)


def dot(left, right):
    return jnp.dot(left, right, preferred_element_type=jnp.float32)


def each(n, body):
    def step(d, carry):
        body(d)
        return carry

    lax.fori_loop(0, n, step, 0)


def kernel(
    nr, nc, fock_hbm, density_hbm, probe_ref, out_ref,
    staged, high, low, vector, blocks, part, swapped, summed,
    load_sem, zs, zr, xs, xr, s1, r1, s2, r2, s3, r3,
):
    r = lax.axis_index("row")
    c = lax.axis_index("col")
    q = nc // nr
    ny = nr // CORES
    y = lax.div(r, CORES)
    k = lax.rem(r, CORES)
    z = lax.div(c, q)
    x = lax.rem(c, q)
    items = STAGES * GROUPS
    chunk = blocks.shape[4]
    group = blocks.shape[3]
    half = group // 2
    pieces = q * CORES
    m = probe_ref.shape[2]
    source = z == r
    goes_up = jnp.logical_and(z >= r, z + 1 < nr)
    goes_down = jnp.logical_and(z <= r, z >= 1)
    sender_offset = jnp.where(z > r, -1, 1)

    def order(i):
        return lax.rem(x + lax.div(i, CORES), q) * CORES + lax.rem(i, CORES)

    def load(matrix, n, index):
        i, side = lax.div(index, 2), lax.rem(index, 2)
        slot = lax.rem(n, SLOTS)
        return pltpu.make_async_copy(
            matrix.at[side, pl.ds(pl.multiple_of(order(i) * chunk, chunk), chunk), :],
            staged.at[slot], load_sem.at[slot],
        )

    total = 2 * pieces

    def start_load(n):
        @pl.when(n < total)
        def _():
            load(fock_hbm, n, n).start()

        @pl.when(jnp.logical_and(n >= total, n < 2 * total))
        def _():
            load(density_hbm, n, n - total).start()

    def take_load(n):
        which = lax.div(n, total)
        index = lax.rem(n, total)
        i, side = lax.div(index, 2), lax.rem(index, 2)
        slot = lax.rem(n, SLOTS)
        load(fock_hbm, n, index).wait()
        rows = min(64, chunk)

        def slab(j):
            where = pl.ds(pl.multiple_of(j * rows, rows), rows)
            target = pl.ds(pl.multiple_of(order(i) * chunk + j * rows, rows), rows)
            top, rest = split(staged[slot, where, :])
            high[which, side, target, :] = top
            low[which, side, target, :] = rest

        each(chunk // rows, slab)
        start_load(n + SLOTS)

    each(SLOTS, start_load)

    barrier = pltpu.get_barrier_semaphore()

    def greet(row, col):
        pl.semaphore_signal(barrier, inc=1, device_id=(row, col), device_id_type=MESH)

    for j in range(1, nr):
        greet(lax.rem(r + j, nr), c)
    for j in range(1, q):
        greet(r, z * q + lax.rem(x + j, q))

    @pl.when(z + 1 < nr)
    def _():
        greet(r, c + q)

    @pl.when(z >= 1)
    def _():
        greet(r, c - q)

    for side in range(2):
        turned = probe_ref[side].T
        for h in range(GROUPS):
            for g in range(CORES):
                vector[0, h, g, side * half:(side + 1) * half, :] = turned[
                    h * half:(h + 1) * half, g * chunk:(g + 1) * chunk
                ]

    neighbours = nr - 1 + q - 1 + jnp.where(z + 1 < nr, 1, 0) + jnp.where(z >= 1, 1, 0)
    pl.semaphore_wait(barrier, neighbours)

    def z_copy(t, g, up):
        return pltpu.make_async_remote_copy(
            src_ref=blocks.at[t, x, g], dst_ref=blocks.at[t, x, g],
            send_sem=zs.at[t, g, up], recv_sem=zr.at[t, g],
            device_id=(r, c + q if up else c - q), device_id_type=MESH,
        )

    def x_copy(t, g, j):
        return pltpu.make_async_remote_copy(
            src_ref=blocks.at[t, x, g], dst_ref=blocks.at[t, x, g],
            send_sem=xs.at[t, g, j], recv_sem=xr.at[t, g, j],
            device_id=(r, z * q + lax.rem(x + 1 + j, q)), device_id_type=MESH,
        )

    def forward(t, g):
        @pl.when(goes_up)
        def _():
            z_copy(t, g, 1).start()

        @pl.when(goes_down)
        def _():
            z_copy(t, g, 0).start()

        for j in range(q - 1):
            x_copy(t, g, j).start()

    def feed(t, g):
        blocks[t, x, g] = vector[lax.div(t, GROUPS), lax.rem(t, GROUPS), g]
        forward(t, g)

    def receive(t, g):
        @pl.when(jnp.logical_not(source))
        def _():
            pltpu.make_async_remote_copy(
                src_ref=blocks.at[t, x, g], dst_ref=blocks.at[t, x, g],
                send_sem=zs.at[t, g, 0], recv_sem=zr.at[t, g],
                device_id=(r, c + sender_offset * q), device_id_type=MESH,
            ).wait_recv()
            forward(t, g)

    @pl.when(source)
    def _():
        def first(h):
            for g in range(CORES):
                feed(h, g)

        each(GROUPS, first)

    def multiply(t, b, g, first):
        stage = lax.div(t, GROUPS)
        which = jnp.where(stage == 1, 1, 0)
        value = blocks[t, b, g]
        top, rest = split(value)
        turned_top = jnp.concatenate([top[half:], -top[:half]], axis=0)
        turned_rest = jnp.concatenate([rest[half:], -rest[:half]], axis=0)
        left = jnp.concatenate([top, rest], axis=0)
        turned_left = jnp.concatenate([turned_top, turned_rest], axis=0)
        rows = pl.ds(pl.multiple_of((b * CORES + g) * chunk, chunk), chunk)
        for o in range(CORES):
            cols = slice(o * chunk, (o + 1) * chunk)
            both = dot(left, high[which, 0, rows, cols]) + dot(turned_left, high[which, 1, rows, cols])
            fine = dot(top, low[which, 0, rows, cols]) + dot(turned_top, low[which, 1, rows, cols])
            value = both[:group] + (both[group:] + fine)
            if first:
                part[t, o] = value
            else:
                part[t, o] += value

    partner = r + 1 - 2 * k
    mine = k
    other = 1 - k

    def swap_copy(t):
        return pltpu.make_async_remote_copy(
            src_ref=part.at[t, other], dst_ref=swapped.at[t],
            send_sem=s1.at[t], recv_sem=r1.at[t],
            device_id=(partner, c), device_id_type=MESH,
        )

    def y_copy(t, j):
        return pltpu.make_async_remote_copy(
            src_ref=summed.at[t, y], dst_ref=summed.at[t, y],
            send_sem=s2.at[t, j], recv_sem=r2.at[t, j],
            device_id=(lax.rem(y + 1 + j, ny) * CORES + k, c), device_id_type=MESH,
        )

    def share_copy(t):
        where = (lax.div(t, GROUPS) + 1, lax.rem(t, GROUPS), mine)
        return pltpu.make_async_remote_copy(
            src_ref=vector.at[where], dst_ref=vector.at[where],
            send_sem=s3.at[t], recv_sem=r3.at[t],
            device_id=(partner, c), device_id_type=MESH,
        )

    def add_cores(t):
        swap_copy(t).wait_recv()
        summed[t, y] = part[t, mine] + swapped[t]
        for j in range(ny - 1):
            y_copy(t, j).start()

    def add_rows(t):
        stage = lax.div(t, GROUPS)
        h = lax.rem(t, GROUPS)
        for j in range(ny - 1):
            y_copy(t, j).wait_recv()
        value = summed[t, 0]
        for j in range(1, ny):
            value = value + summed[t, j]
        factor = jnp.where(stage == 0, time_step, jnp.where(stage == 2, -time_step, 0.0)).astype(jnp.float32)
        keep = jnp.where(stage == 1, 0.0, 1.0).astype(jnp.float32)
        plain = jnp.where(stage == 1, 1.0, 0.0).astype(jnp.float32)
        old = vector[stage, h, mine]
        vector[stage + 1, h, mine, :half, :] = keep * old[:half] + (plain * value[:half] - factor * value[half:])
        vector[stage + 1, h, mine, half:, :] = keep * old[half:] + (plain * value[half:] + factor * value[:half])
        share_copy(t).start()
        feed_next(t, mine)

    def take_share(t):
        share_copy(t).wait_recv()
        feed_next(t, other)

    def feed_next(t, g):
        @pl.when(jnp.logical_and(source, t + GROUPS < items))
        def _():
            feed(t + GROUPS, g)

    per_slot = pieces // GROUPS

    def slot(t):
        def ready(i):
            @pl.when(t == 0)
            def _():
                take_load(2 * i)
                take_load(2 * i + 1)

        receive(t, 0)

        @pl.when(t >= 1)
        def _():
            add_cores(t - 1)

        ready(0)
        multiply(t, x, 0, True)
        receive(t, 1)
        ready(1)
        multiply(t, x, 1, False)

        @pl.when(t >= 2)
        def _():
            add_rows(t - 2)

        for i in range(1, q):
            for g in range(CORES):
                ready(i * CORES + g)
                x_copy(t, g, q - 1 - i).wait_recv()
                multiply(t, lax.rem(x + i, q), g, False)

        swap_copy(t).start()

        @pl.when(t >= 2)
        def _():
            take_share(t - 2)

        @pl.when(t < GROUPS)
        def _():
            for i in range(per_slot):
                for side in range(2):
                    take_load(total + 2 * (t * per_slot + i) + side)

    each(items, slot)

    last = items - 1
    add_cores(last)
    add_rows(last - 1)
    take_share(last - 1)
    add_rows(last)
    take_share(last)

    for side in range(2):
        for g in range(CORES):
            whole = jnp.concatenate(
                [vector[STAGES, h, g, side * half:(side + 1) * half, :] for h in range(GROUPS)], axis=0
            )
            out_ref[side, g * chunk:(g + 1) * chunk, :] = whole.T

    def drain(t):
        for g in range(CORES):
            @pl.when(goes_up)
            def _():
                z_copy(t, g, 1).wait_send()

            @pl.when(goes_down)
            def _():
                z_copy(t, g, 0).wait_send()

            for j in range(q - 1):
                x_copy(t, g, j).wait_send()
        swap_copy(t).wait_send()
        for j in range(ny - 1):
            y_copy(t, j).wait_send()
        share_copy(t).wait_send()

    each(items, drain)


def solution(mesh):
    nr = mesh.shape["row"]
    nc = mesh.shape["col"]

    def shards(fock, density, probe):
        _, rows, cols = fock.shape
        m = probe.shape[2]
        q = nc // nr
        ny = nr // CORES
        group = 2 * m // GROUPS
        chunk = cols // CORES
        items = STAGES * GROUPS
        f32 = jnp.float32
        bf16 = jnp.bfloat16
        vmem = pltpu.VMEM
        sem = pltpu.SemaphoreType.DMA
        others = max(q - 1, 1)
        far = max(ny - 1, 1)
        return pl.pallas_call(
            functools.partial(kernel, nr, nc),
            out_shape=jax.ShapeDtypeStruct(probe.shape, f32),
            in_specs=[
                pl.BlockSpec(memory_space=pl.ANY),
                pl.BlockSpec(memory_space=pl.ANY),
                pl.BlockSpec(memory_space=pltpu.VMEM),
            ],
            out_specs=pl.BlockSpec(memory_space=pltpu.VMEM),
            scratch_shapes=[
                vmem((SLOTS, chunk, cols), f32),
                vmem((2, 2, rows, cols), bf16),
                vmem((2, 2, rows, cols), bf16),
                vmem((STAGES + 1, GROUPS, CORES, group, chunk), f32),
                vmem((items, q, CORES, group, chunk), f32),
                vmem((items, CORES, group, chunk), f32),
                vmem((items, group, chunk), f32),
                vmem((items, ny, group, chunk), f32),
                sem((SLOTS,)),
                sem((items, CORES, 2)),
                sem((items, CORES)),
                sem((items, CORES, others)),
                sem((items, CORES, others)),
                sem((items,)),
                sem((items,)),
                sem((items, far)),
                sem((items, far)),
                sem((items,)),
                sem((items,)),
            ],
            compiler_params=pltpu.CompilerParams(
                collective_id=0, has_side_effects=True, vmem_limit_bytes=63 * 1024 * 1024
            ),
            name="propagate",
        )(fock, density, probe)

    return jax.shard_map(
        shards,
        mesh=mesh,
        in_specs=(P(None, "row", "col"), P(None, "row", "col"), P(None, "col", None)),
        out_specs=P(None, "col", None),
        check_vma=False,
    )
```

time: 150 us -> 129 us (0.86)
  the two profiles are of different devices: /device:TPU:15 before, /device:TPU:0 now
where the time goes in v1:
time: 129 us
  Pallas kernels  127 us (98%)
  local copies, waits for them, and re-layouts  2.26 us (2%)
    pallas_call x1, Pallas kernels, shards(): pl.pallas_call(functools.partial(kernel, nr, nc), out_shape=jax.ShapeDtyp...  127 us

profile of v1, /device:TPU:0, one launch (start us, length us, event | category | flops | bytes accessed | tf_op | source)
XLA Modules:
  0.0 128.9 jit_solution(6563049543617704255)
XLA Ops:
  0.0 126.7 %propagate.1 = f32[2,1024,128]{2,1,0:T(8,128)} custom-call(f32[2,2048,1024]{2,1,0:T(8,128)} %fock_hbm.1, f32[2,2048,1024]{2,1,0:T(8,128)} %density_hbm.1, f32[2,1024,128]{2,1,0:T(8,128)} %probe_ref.1), custom_call_target="tpu_custom_call" | custom-call | tf_op jit(solution)/shard_map/propagate/pallas_call | solution.py:353
  126.7 2.3 %copy.5 = f32[2,1024,128]{2,1,0:T(8,128)} copy(f32[2,1024,128]{2,1,0:T(8,128)} %propagate.1) | data formatting | bytes 2097152

commit v2 on v1

--- a/solution.py
+++ b/solution.py
@@ -51,13 +51,21 @@
     half = group // 2
     pieces = q * CORES
     m = probe_ref.shape[2]
+    cut = 1
+    bits = CORES * cut
+    width = chunk // cut
     source = z == r
-    goes_up = jnp.logical_and(z >= r, z + 1 < nr)
-    goes_down = jnp.logical_and(z <= r, z >= 1)
-    sender_offset = jnp.where(z > r, -1, 1)
+    ends = jnp.logical_or(r == 0, r == nr - 1)
+    near = jnp.logical_and(ends, jnp.logical_or(z == r + 1, z == r - 1))
+    goes_up = jnp.logical_and(jnp.logical_and(z >= r, z + 1 < nr), jnp.logical_not(near))
+    goes_down = jnp.logical_and(jnp.logical_and(z <= r, z >= 1), jnp.logical_not(near))
+    far_step = jnp.where(r == 0, 2, -2)
+    goes_far = jnp.logical_and(jnp.logical_and(ends, source), nr > 2)
 
     def order(i):
-        return lax.rem(x + lax.div(i, CORES), q) * CORES + lax.rem(i, CORES)
+        b = jnp.where(i < 2, 0, 1 + lax.rem(i - 2, max(q - 1, 1)))
+        g = jnp.where(i < 2, i, lax.div(i - 2, max(q - 1, 1)))
+        return lax.rem(x + b, q) * CORES + g
 
     def load(matrix, n, index):
         i, side = lax.div(index, 2), lax.rem(index, 2)
@@ -116,6 +124,14 @@
     def _():
         greet(r, c - q)
 
+    @pl.when(z + 2 < nr)
+    def _():
+        greet(r, c + 2 * q)
+
+    @pl.when(z >= 2)
+    def _():
+        greet(r, c - 2 * q)
+
     for side in range(2):
         turned = probe_ref[side].T
         for h in range(GROUPS):
@@ -124,48 +140,64 @@
                     h * half:(h + 1) * half, g * chunk:(g + 1) * chunk
                 ]
 
-    neighbours = nr - 1 + q - 1 + jnp.where(z + 1 < nr, 1, 0) + jnp.where(z >= 1, 1, 0)
+    neighbours = nr - 1 + q - 1
+    for step in (1, 2):
+        neighbours += jnp.where(z + step < nr, 1, 0) + jnp.where(z >= step, 1, 0)
     pl.semaphore_wait(barrier, neighbours)
 
-    def z_copy(t, g, up):
+    def bit(t, b):
+        g, w = b // cut, b % cut
+        return blocks.at[t, x, g, :, pl.ds(w * width, width)]
+
+    def z_copy(t, b, way, step):
         return pltpu.make_async_remote_copy(
-            src_ref=blocks.at[t, x, g], dst_ref=blocks.at[t, x, g],
-            send_sem=zs.at[t, g, up], recv_sem=zr.at[t, g],
-            device_id=(r, c + q if up else c - q), device_id_type=MESH,
-        )
-
-    def x_copy(t, g, j):
+            src_ref=bit(t, b), dst_ref=bit(t, b),
+            send_sem=zs.at[t, b, way], recv_sem=zr.at[t, b],
+            device_id=(r, c + step * q), device_id_type=MESH,
+        )
+
+    def x_copy(t, b, j):
         return pltpu.make_async_remote_copy(
-            src_ref=blocks.at[t, x, g], dst_ref=blocks.at[t, x, g],
-            send_sem=xs.at[t, g, j], recv_sem=xr.at[t, g, j],
+            src_ref=bit(t, b), dst_ref=bit(t, b),
+            send_sem=xs.at[t, b, j], recv_sem=xr.at[t, b, j],
             device_id=(r, z * q + lax.rem(x + 1 + j, q)), device_id_type=MESH,
         )
 
-    def forward(t, g):
+    def each_z(t, b, act):
+        @pl.when(goes_far)
+        def _():
+            act(z_copy(t, b, 2, far_step))
+
         @pl.when(goes_up)
         def _():
-            z_copy(t, g, 1).start()
+            act(z_copy(t, b, 1, 1))
 
         @pl.when(goes_down)
         def _():
-            z_copy(t, g, 0).start()
-
+            act(z_copy(t, b, 0, -1))
+
+    def forward(t, b):
+        each_z(t, b, lambda copy: copy.start())
         for j in range(q - 1):
-            x_copy(t, g, j).start()
+            x_copy(t, b, j).start()
 
     def feed(t, g):
         blocks[t, x, g] = vector[lax.div(t, GROUPS), lax.rem(t, GROUPS), g]
-        forward(t, g)
-
-    def receive(t, g):
+        if isinstance(g, int):
+            for w in range(cut):
+                forward(t, g * cut + w)
+        else:
+            for value in range(CORES):
+                @pl.when(g == value)
+                def _():
+                    for w in range(cut):
+                        forward(t, value * cut + w)
+
+    def receive(t, b):
         @pl.when(jnp.logical_not(source))
         def _():
-            pltpu.make_async_remote_copy(
-                src_ref=blocks.at[t, x, g], dst_ref=blocks.at[t, x, g],
-                send_sem=zs.at[t, g, 0], recv_sem=zr.at[t, g],
-                device_id=(r, c + sender_offset * q), device_id_type=MESH,
-            ).wait_recv()
-            forward(t, g)
+            z_copy(t, b, 0, jnp.where(z > r, -1, 1)).wait_recv()
+            forward(t, b)
 
     @pl.when(source)
     def _():
@@ -175,7 +207,11 @@
 
         each(GROUPS, first)
 
-    def multiply(t, b, g, first):
+    partner = r + 1 - 2 * k
+    mine = k
+    other = 1 - k
+
+    def multiply(t, b, g, first, between=None):
         stage = lax.div(t, GROUPS)
         which = jnp.where(stage == 1, 1, 0)
         value = blocks[t, b, g]
@@ -185,8 +221,8 @@
         left = jnp.concatenate([top, rest], axis=0)
         turned_left = jnp.concatenate([turned_top, turned_rest], axis=0)
         rows = pl.ds(pl.multiple_of((b * CORES + g) * chunk, chunk), chunk)
-        for o in range(CORES):
-            cols = slice(o * chunk, (o + 1) * chunk)
+        for o in (other, mine):
+            cols = pl.ds(pl.multiple_of(o * chunk, chunk), chunk)
             both = dot(left, high[which, 0, rows, cols]) + dot(turned_left, high[which, 1, rows, cols])
             fine = dot(top, low[which, 0, rows, cols]) + dot(turned_top, low[which, 1, rows, cols])
             value = both[:group] + (both[group:] + fine)
@@ -194,10 +230,8 @@
                 part[t, o] = value
             else:
                 part[t, o] += value
-
-    partner = r + 1 - 2 * k
-    mine = k
-    other = 1 - k
+            if between is not None and o is other:
+                between()
 
     def swap_copy(t):
         return pltpu.make_async_remote_copy(
@@ -253,54 +287,111 @@
         def _():
             feed(t + GROUPS, g)
 
-    per_slot = pieces // GROUPS
+    points = 2 * (GROUPS - 2)
+    per_point = -(-total // points)
+    rest = CORES - 1
+
+    def take_fock(i):
+        take_load(2 * i)
+        take_load(2 * i + 1)
+
+    def take_density(point):
+        def one(i):
+            n = total + point * per_point + i
+
+            @pl.when(n < 2 * total)
+            def _():
+                take_load(n)
+
+        each(per_point, one)
+
+    def wait_x(t, g, i):
+        x_copy(t, g, q - 1 - i).wait_recv()
+
+    def finish(t):
+        for i in range(1, q):
+            wait_x(t, rest, i)
+            last_one = i == q - 1
+            multiply(t, lax.rem(x + i, q), rest, False, (lambda: swap_copy(t).start()) if last_one else None)
+
+    def cross(t):
+        for i in range(1, q):
+            wait_x(t, 0, i)
+            multiply(t, lax.rem(x + i, q), 0, False)
 
     def slot(t):
-        def ready(i):
-            @pl.when(t == 0)
-            def _():
-                take_load(2 * i)
-                take_load(2 * i + 1)
+        filling = jnp.logical_and(t >= 2, t < GROUPS)
+
+        @pl.when(t == 1)
+        def _():
+            take_fock(0)
+
+        @pl.when(t >= 1)
+        def _():
+            multiply(t - 1, x, 0, True)
+
+        @pl.when(t == 1)
+        def _():
+            take_fock(1)
+
+        @pl.when(t >= 1)
+        def _():
+            multiply(t - 1, x, 1, False)
+
+        @pl.when(t >= 3)
+        def _():
+            add_rows(t - 3)
+
+        @pl.when(t >= 2)
+        def _():
+            add_cores(t - 2)
+
+        @pl.when(t == 1)
+        def _():
+            for i in range(1, q):
+                take_fock(q - 1 + i)
+
+        @pl.when(t >= 1)
+        def _():
+            cross(t - 1)
 
         receive(t, 0)
 
+        @pl.when(t >= 3)
+        def _():
+            take_share(t - 3)
+
+        @pl.when(filling)
+        def _():
+            take_density(2 * (t - 2) + 0)
+
+        @pl.when(t == 1)
+        def _():
+            for i in range(1, q):
+                take_fock(q + i)
+
         @pl.when(t >= 1)
         def _():
-            add_cores(t - 1)
-
-        ready(0)
-        multiply(t, x, 0, True)
+            finish(t - 1)
+
         receive(t, 1)
-        ready(1)
-        multiply(t, x, 1, False)
-
-        @pl.when(t >= 2)
-        def _():
-            add_rows(t - 2)
-
-        for i in range(1, q):
-            for g in range(CORES):
-                ready(i * CORES + g)
-                x_copy(t, g, q - 1 - i).wait_recv()
-                multiply(t, lax.rem(x + i, q), g, False)
-
-        swap_copy(t).start()
-
-        @pl.when(t >= 2)
-        def _():
-            take_share(t - 2)
-
-        @pl.when(t < GROUPS)
-        def _():
-            for i in range(per_slot):
-                for side in range(2):
-                    take_load(total + 2 * (t * per_slot + i) + side)
+
+        @pl.when(filling)
+        def _():
+            take_density(2 * (t - 2) + 1)
 
     each(items, slot)
 
     last = items - 1
+    multiply(last, x, 0, True)
+    multiply(last, x, 1, False)
+    add_rows(last - 2)
+    add_cores(last - 1)
+    cross(last)
+    take_share(last - 2)
+    finish(last)
+    add_rows(last - 1)
     add_cores(last)
-    add_rows(last - 1)
     take_share(last - 1)
     add_rows(last)
     take_share(last)
@@ -313,17 +404,10 @@
             out_ref[side, g * chunk:(g + 1) * chunk, :] = whole.T
 
     def drain(t):
-        for g in range(CORES):
-            @pl.when(goes_up)
-            def _():
-                z_copy(t, g, 1).wait_send()
-
-            @pl.when(goes_down)
-            def _():
-                z_copy(t, g, 0).wait_send()
-
+        for b in range(bits):
+            each_z(t, b, lambda copy: copy.wait_send())
             for j in range(q - 1):
-                x_copy(t, g, j).wait_send()
+                x_copy(t, b, j).wait_send()
         swap_copy(t).wait_send()
         for j in range(ny - 1):
             y_copy(t, j).wait_send()
@@ -344,6 +428,7 @@
         group = 2 * m // GROUPS
         chunk = cols // CORES
         items = STAGES * GROUPS
+        bits = CORES
         f32 = jnp.float32
         bf16 = jnp.bfloat16
         vmem = pltpu.VMEM
@@ -369,10 +454,10 @@
                 vmem((items, group, chunk), f32),
                 vmem((items, ny, group, chunk), f32),
                 sem((SLOTS,)),
-                sem((items, CORES, 2)),
-                sem((items, CORES)),
-                sem((items, CORES, others)),
-                sem((items, CORES, others)),
+                sem((items, bits, 3)),
+                sem((items, bits)),
+                sem((items, bits, others)),
+                sem((items, bits, others)),
                 sem((items,)),
                 sem((items,)),
                 sem((items, far)),

time: 129 us -> 104 us (0.81)
  Pallas kernels: 127 us -> 101 us
    pallas_call x1, Pallas kernels: 127 us -> 101 us  [shards(): pl.pallas_call(functools.partial(kernel, nr, nc), out_shape=jax.ShapeDtyp...]
where the time goes in v2:
time: 104 us
  Pallas kernels  101 us (97%)
  local copies, waits for them, and re-layouts  2.26 us (2%)
    pallas_call x1, Pallas kernels, shards(): pl.pallas_call(functools.partial(kernel, nr, nc), out_shape=jax.ShapeDtyp...  101 us
    unnamed x1, local copies, waits for them, and re-layouts  2.26 us

profile of v2, /device:TPU:0, one launch (start us, length us, event | category | flops | bytes accessed | tf_op | source)
XLA Modules:
  0.0 103.6 jit_solution(8301612619484594789)
XLA Ops:
  0.0 101.4 %propagate.1 = f32[2,1024,128]{2,1,0:T(8,128)} custom-call(f32[2,2048,1024]{2,1,0:T(8,128)} %fock_hbm.1, f32[2,2048,1024]{2,1,0:T(8,128)} %density_hbm.1, f32[2,1024,128]{2,1,0:T(8,128)} %probe_ref.1), custom_call_target="tpu_custom_call" | custom-call | tf_op jit(solution)/shard_map/propagate/pallas_call | solution.py:438
  101.4 2.3 %copy.5 = f32[2,1024,128]{2,1,0:T(8,128)} copy(f32[2,1024,128]{2,1,0:T(8,128)} %propagate.1) | data formatting | bytes 2097152

commit v3 on v2

--- a/solution.py
+++ b/solution.py
@@ -35,7 +35,7 @@
 def kernel(
     nr, nc, fock_hbm, density_hbm, probe_ref, out_ref,
     staged, high, low, vector, blocks, part, swapped, summed,
-    load_sem, zs, zr, xs, xr, s1, r1, s2, r2, s3, r3,
+    load_sem, zs, zr, xs, xr, hs, s1, r1, s2, r2, s3, r3,
 ):
     r = lax.axis_index("row")
     c = lax.axis_index("col")
@@ -51,16 +51,19 @@
     half = group // 2
     pieces = q * CORES
     m = probe_ref.shape[2]
-    cut = 1
-    bits = CORES * cut
-    width = chunk // cut
     source = z == r
     ends = jnp.logical_or(r == 0, r == nr - 1)
-    near = jnp.logical_and(ends, jnp.logical_or(z == r + 1, z == r - 1))
+    near = jnp.logical_and(ends, jnp.logical_or(z == r + 1, z == r - 1)) if nr > 2 else r < 0
     goes_up = jnp.logical_and(jnp.logical_and(z >= r, z + 1 < nr), jnp.logical_not(near))
     goes_down = jnp.logical_and(jnp.logical_and(z <= r, z >= 1), jnp.logical_not(near))
-    far_step = jnp.where(r == 0, 2, -2)
-    goes_far = jnp.logical_and(jnp.logical_and(ends, source), nr > 2)
+    def twin(row):
+        return lax.rem(lax.div(row, CORES) + 1, ny) * CORES + lax.rem(row, CORES)
+
+    helped = nr > 2 and ny > 1
+    at_end = jnp.logical_or(z == 0, z == nr - 1)
+    assists = jnp.logical_and(at_end, r == twin(z)) if helped else r < 0
+    assisted = c + jnp.where(z == 0, 2, -2) * q
+    second = jnp.logical_and(ends, jnp.logical_or(z == r + 2, z == r - 2)) if helped else r < 0
 
     def order(i):
         b = jnp.where(i < 2, 0, 1 + lax.rem(i - 2, max(q - 1, 1)))
@@ -124,13 +127,13 @@
     def _():
         greet(r, c - q)
 
-    @pl.when(z + 2 < nr)
+    @pl.when(assists)
     def _():
-        greet(r, c + 2 * q)
-
-    @pl.when(z >= 2)
+        greet(z, assisted)
+
+    @pl.when(second)
     def _():
-        greet(r, c - 2 * q)
+        greet(twin(r), r * q + x)
 
     for side in range(2):
         turned = probe_ref[side].T
@@ -141,71 +144,66 @@
                 ]
 
     neighbours = nr - 1 + q - 1
-    for step in (1, 2):
-        neighbours += jnp.where(z + step < nr, 1, 0) + jnp.where(z >= step, 1, 0)
+    for meets in (z + 1 < nr, z >= 1, assists, second):
+        neighbours += jnp.where(meets, 1, 0)
     pl.semaphore_wait(barrier, neighbours)
 
-    def bit(t, b):
-        g, w = b // cut, b % cut
-        return blocks.at[t, x, g, :, pl.ds(w * width, width)]
-
-    def z_copy(t, b, way, step):
-        return pltpu.make_async_remote_copy(
-            src_ref=bit(t, b), dst_ref=bit(t, b),
-            send_sem=zs.at[t, b, way], recv_sem=zr.at[t, b],
+    def z_copy(t, g, up, step):
+        return pltpu.make_async_remote_copy(
+            src_ref=blocks.at[t, x, g], dst_ref=blocks.at[t, x, g],
+            send_sem=zs.at[t, g, up], recv_sem=zr.at[t, g],
             device_id=(r, c + step * q), device_id_type=MESH,
         )
 
-    def x_copy(t, b, j):
-        return pltpu.make_async_remote_copy(
-            src_ref=bit(t, b), dst_ref=bit(t, b),
-            send_sem=xs.at[t, b, j], recv_sem=xr.at[t, b, j],
+    def x_copy(t, g, j):
+        return pltpu.make_async_remote_copy(
+            src_ref=blocks.at[t, x, g], dst_ref=blocks.at[t, x, g],
+            send_sem=xs.at[t, g, j], recv_sem=xr.at[t, g, j],
             device_id=(r, z * q + lax.rem(x + 1 + j, q)), device_id_type=MESH,
         )
 
-    def each_z(t, b, act):
-        @pl.when(goes_far)
-        def _():
-            act(z_copy(t, b, 2, far_step))
-
+    def assist_copy(t, g):
+        return pltpu.make_async_remote_copy(
+            src_ref=vector.at[lax.div(t, GROUPS), lax.rem(t, GROUPS), g], dst_ref=blocks.at[t, x, g],
+            send_sem=hs.at[t, g], recv_sem=zr.at[t, g],
+            device_id=(z, assisted), device_id_type=MESH,
+        )
+
+    def each_z(t, g, act):
         @pl.when(goes_up)
         def _():
-            act(z_copy(t, b, 1, 1))
+            act(z_copy(t, g, 1, 1))
 
         @pl.when(goes_down)
         def _():
-            act(z_copy(t, b, 0, -1))
-
-    def forward(t, b):
-        each_z(t, b, lambda copy: copy.start())
+            act(z_copy(t, g, 0, -1))
+
+    def forward(t, g):
+        each_z(t, g, lambda copy: copy.start())
         for j in range(q - 1):
-            x_copy(t, b, j).start()
+            x_copy(t, g, j).start()
 
     def feed(t, g):
-        blocks[t, x, g] = vector[lax.div(t, GROUPS), lax.rem(t, GROUPS), g]
-        if isinstance(g, int):
-            for w in range(cut):
-                forward(t, g * cut + w)
-        else:
-            for value in range(CORES):
-                @pl.when(g == value)
-                def _():
-                    for w in range(cut):
-                        forward(t, value * cut + w)
-
-    def receive(t, b):
+        @pl.when(source)
+        def _():
+            blocks[t, x, g] = vector[lax.div(t, GROUPS), lax.rem(t, GROUPS), g]
+            forward(t, g)
+
+        @pl.when(assists)
+        def _():
+            assist_copy(t, g).start()
+
+    def receive(t, g):
         @pl.when(jnp.logical_not(source))
         def _():
-            z_copy(t, b, 0, jnp.where(z > r, -1, 1)).wait_recv()
-            forward(t, b)
-
-    @pl.when(source)
-    def _():
-        def first(h):
-            for g in range(CORES):
-                feed(h, g)
-
-        each(GROUPS, first)
+            z_copy(t, g, 0, jnp.where(z > r, -1, 1)).wait_recv()
+            forward(t, g)
+
+    def first(h):
+        for g in range(CORES):
+            feed(h, g)
+
+    each(GROUPS, first)
 
     partner = r + 1 - 2 * k
     mine = k
@@ -283,7 +281,7 @@
         feed_next(t, other)
 
     def feed_next(t, g):
-        @pl.when(jnp.logical_and(source, t + GROUPS < items))
+        @pl.when(t + GROUPS < items)
         def _():
             feed(t + GROUPS, g)
 
@@ -322,29 +320,17 @@
     def slot(t):
         filling = jnp.logical_and(t >= 2, t < GROUPS)
 
+        @pl.when(t >= 2)
+        def _():
+            add_cores(t - 2)
+
         @pl.when(t == 1)
         def _():
-            take_fock(0)
+            take_fock(1)
 
         @pl.when(t >= 1)
         def _():
-            multiply(t - 1, x, 0, True)
-
-        @pl.when(t == 1)
-        def _():
-            take_fock(1)
-
-        @pl.when(t >= 1)
-        def _():
             multiply(t - 1, x, 1, False)
-
-        @pl.when(t >= 3)
-        def _():
-            add_rows(t - 3)
-
-        @pl.when(t >= 2)
-        def _():
-            add_cores(t - 2)
 
         @pl.when(t == 1)
         def _():
@@ -355,15 +341,21 @@
         def _():
             cross(t - 1)
 
+        @pl.when(t >= 3)
+        def _():
+            take_share(t - 3)
+
         receive(t, 0)
 
-        @pl.when(t >= 3)
-        def _():
-            take_share(t - 3)
-
         @pl.when(filling)
         def _():
             take_density(2 * (t - 2) + 0)
+
+        @pl.when(t == 0)
+        def _():
+            take_fock(0)
+
+        multiply(t, x, 0, True)
 
         @pl.when(t == 1)
         def _():
@@ -376,6 +368,10 @@
 
         receive(t, 1)
 
+        @pl.when(t >= 2)
+        def _():
+            add_rows(t - 2)
+
         @pl.when(filling)
         def _():
             take_density(2 * (t - 2) + 1)
@@ -383,10 +379,8 @@
     each(items, slot)
 
     last = items - 1
-    multiply(last, x, 0, True)
+    add_cores(last - 1)
     multiply(last, x, 1, False)
-    add_rows(last - 2)
-    add_cores(last - 1)
     cross(last)
     take_share(last - 2)
     finish(last)
@@ -404,10 +398,14 @@
             out_ref[side, g * chunk:(g + 1) * chunk, :] = whole.T
 
     def drain(t):
-        for b in range(bits):
-            each_z(t, b, lambda copy: copy.wait_send())
+        for g in range(CORES):
+            each_z(t, g, lambda copy: copy.wait_send())
             for j in range(q - 1):
-                x_copy(t, b, j).wait_send()
+                x_copy(t, g, j).wait_send()
+
+            @pl.when(assists)
+            def _():
+                assist_copy(t, g).wait_send()
         swap_copy(t).wait_send()
         for j in range(ny - 1):
             y_copy(t, j).wait_send()
@@ -428,7 +426,6 @@
         group = 2 * m // GROUPS
         chunk = cols // CORES
         items = STAGES * GROUPS
-        bits = CORES
         f32 = jnp.float32
         bf16 = jnp.bfloat16
         vmem = pltpu.VMEM
@@ -454,10 +451,11 @@
                 vmem((items, group, chunk), f32),
                 vmem((items, ny, group, chunk), f32),
                 sem((SLOTS,)),
-                sem((items, bits, 3)),
-                sem((items, bits)),
-                sem((items, bits, others)),
-                sem((items, bits, others)),
+                sem((items, CORES, 2)),
+                sem((items, CORES)),
+                sem((items, CORES, others)),
+                sem((items, CORES, others)),
+                sem((items, CORES)),
                 sem((items,)),
                 sem((items,)),
                 sem((items, far)),

time: 104 us -> 103 us (level)
  no operation moved by 1% of the time
where the time goes in v3:
time: 103 us
  Pallas kernels  101 us (98%)
  local copies, waits for them, and re-layouts  2.26 us (2%)
    pallas_call x1, Pallas kernels, shards(): pl.pallas_call(functools.partial(kernel, nr, nc), out_shape=jax.ShapeDtyp...  101 us
    unnamed x1, local copies, waits for them, and re-layouts  2.26 us

profile of v3, /device:TPU:0, one launch (start us, length us, event | category | flops | bytes accessed | tf_op | source)
XLA Modules:
  0.0 102.8 jit_solution(7554872798072339985)
XLA Ops:
  0.0 100.6 %propagate.1 = f32[2,1024,128]{2,1,0:T(8,128)} custom-call(f32[2,2048,1024]{2,1,0:T(8,128)} %fock_hbm.1, f32[2,2048,1024]{2,1,0:T(8,128)} %density_hbm.1, f32[2,1024,128]{2,1,0:T(8,128)} %probe_ref.1), custom_call_target="tpu_custom_call" | custom-call | tf_op jit(solution)/shard_map/propagate/pallas_call | solution.py:435
  100.6 2.3 %copy.5 = f32[2,1024,128]{2,1,0:T(8,128)} copy(f32[2,1024,128]{2,1,0:T(8,128)} %propagate.1) | data formatting | bytes 2097152

commit v4 on v3

--- a/solution.py
+++ b/solution.py
@@ -53,7 +53,8 @@
     m = probe_ref.shape[2]
     source = z == r
     ends = jnp.logical_or(r == 0, r == nr - 1)
-    near = jnp.logical_and(ends, jnp.logical_or(z == r + 1, z == r - 1)) if nr > 2 else r < 0
+    inner = jnp.logical_not(ends)
+    near = jnp.logical_or(z == r + 1, z == r - 1) if nr > 2 else r < 0
     goes_up = jnp.logical_and(jnp.logical_and(z >= r, z + 1 < nr), jnp.logical_not(near))
     goes_down = jnp.logical_and(jnp.logical_and(z <= r, z >= 1), jnp.logical_not(near))
     def twin(row):
@@ -64,6 +65,11 @@
     assists = jnp.logical_and(at_end, r == twin(z)) if helped else r < 0
     assisted = c + jnp.where(z == 0, 2, -2) * q
     second = jnp.logical_and(ends, jnp.logical_or(z == r + 2, z == r - 2)) if helped else r < 0
+
+    far_up = jnp.logical_and(jnp.logical_and(source, inner), z + 2 < nr)
+    far_down = jnp.logical_and(jnp.logical_and(source, inner), z >= 2)
+    from_below = jnp.logical_and(inner, z == r + 2)
+    from_above = jnp.logical_and(inner, z == r - 2)
 
     def order(i):
         b = jnp.where(i < 2, 0, 1 + lax.rem(i - 2, max(q - 1, 1)))
@@ -135,6 +141,14 @@
     def _():
         greet(twin(r), r * q + x)
 
+    @pl.when(jnp.logical_or(far_up, from_above))
+    def _():
+        greet(r, c + 2 * q)
+
+    @pl.when(jnp.logical_or(far_down, from_below))
+    def _():
+        greet(r, c - 2 * q)
+
     for side in range(2):
         turned = probe_ref[side].T
         for h in range(GROUPS):
@@ -144,7 +158,7 @@
                 ]
 
     neighbours = nr - 1 + q - 1
-    for meets in (z + 1 < nr, z >= 1, assists, second):
+    for meets in (z + 1 < nr, z >= 1, assists, second, far_up, far_down, from_below, from_above):
         neighbours += jnp.where(meets, 1, 0)
     pl.semaphore_wait(barrier, neighbours)
 
@@ -170,6 +184,14 @@
         )
 
     def each_z(t, g, act):
+        @pl.when(far_up)
+        def _():
+            act(z_copy(t, g, 3, 2))
+
+        @pl.when(far_down)
+        def _():
+            act(z_copy(t, g, 2, -2))
+
         @pl.when(goes_up)
         def _():
             act(z_copy(t, g, 1, 1))
@@ -451,7 +473,7 @@
                 vmem((items, group, chunk), f32),
                 vmem((items, ny, group, chunk), f32),
                 sem((SLOTS,)),
-                sem((items, CORES, 2)),
+                sem((items, CORES, 4)),
                 sem((items, CORES)),
                 sem((items, CORES, others)),
                 sem((items, CORES, others)),

time: 103 us -> 103 us (level)
  no operation moved by 1% of the time
where the time goes in v4:
time: 103 us; the launch traced here: 102 us
  Pallas kernels  100 us (97%)
  local copies, waits for them, and re-layouts  2.26 us (2%)
    pallas_call x1, Pallas kernels, shards(): pl.pallas_call(functools.partial(kernel, nr, nc), out_shape=jax.ShapeDtyp...  100 us
    unnamed x1, local copies, waits for them, and re-layouts  2.26 us

profile of v4, /device:TPU:0, one launch (start us, length us, event | category | flops | bytes accessed | tf_op | source)
XLA Modules:
  0.0 102.3 jit_solution(4661219659864025196)
XLA Ops:
  0.0 100.0 %propagate.1 = f32[2,1024,128]{2,1,0:T(8,128)} custom-call(f32[2,2048,1024]{2,1,0:T(8,128)} %fock_hbm.1, f32[2,2048,1024]{2,1,0:T(8,128)} %density_hbm.1, f32[2,1024,128]{2,1,0:T(8,128)} %probe_ref.1), custom_call_target="tpu_custom_call" | custom-call | tf_op jit(solution)/shard_map/propagate/pallas_call | solution.py:457
  100.0 2.3 %copy.5 = f32[2,1024,128]{2,1,0:T(8,128)} copy(f32[2,1024,128]{2,1,0:T(8,128)} %propagate.1) | data formatting | bytes 2097152
